TPU v7x, 8 devices: a whole 2x2x1 slice. The times are simulated.
8 devices in a mesh: dp: 1 (over z), vp: 8 (over y, x, core).
Axes of the slice: x: 2, y: 2, z: 1, core: 2. Of those that a mesh axis runs over, the one named last changes fastest.
Arguments:
- hidden: bfloat16 [128, 32, 4096], P('vp', 'dp')
- norm_gain: float32 [4096], replicated
- norm_bias: float32 [4096], replicated
- w_out: bfloat16 [4096, 51200], P(None, 'vp')
- labels: int32 [128, 32], P('vp', 'dp')
- loss_mask: float32 [128, 32], P('vp', 'dp')
Outputs:
- output 1: float32 [1], P('dp')
- output 2: bfloat16 [128, 32, 4096], P('vp', 'dp')
- output 3: float32 [4096, 51200], P('dp', 'vp')
- output 4: float32 [4096], P('dp')
- output 5: float32 [4096], P('dp')
All inputs are finite; a program needn't handle non-finite values.
Results may differ from a plain program's by a relative error of at most 0.001.
Values are sent between devices in bfloat16 or wider.
A program may use at most 1 GiB of HBM per device.

v0:
```python
import jax
import jax.numpy as jnp
from jax import lax
from jax.sharding import PartitionSpec as P

NORM_EPS = 1e-5


def norm_forward(hidden, norm_gain, norm_bias):
    x_float = hidden.astype(jnp.float32)
    tok_mean = jnp.mean(x_float, axis=-1, keepdims=True)
    centered = x_float - tok_mean
    inv_std = lax.rsqrt(jnp.mean(centered * centered, axis=-1, keepdims=True) + NORM_EPS)
    normed = centered * inv_std
    h_bf = (normed * (1.0 + norm_gain) + norm_bias).astype(jnp.bfloat16)
    return h_bf, normed, inv_std


def norm_backward(grad_h, normed, inv_std, norm_gain):
    scaled = grad_h * (1.0 + norm_gain)
    centered_grad = scaled - jnp.mean(scaled, axis=-1, keepdims=True)
    return (inv_std * (centered_grad - normed * jnp.mean(scaled * normed, axis=-1, keepdims=True))).astype(jnp.bfloat16)


def solution(mesh):
    def per_device(hidden, norm_gain, norm_bias, w_blk, labels, loss_mask):
        h_bf, normed, inv_std = norm_forward(hidden, norm_gain, norm_bias)
        h_all = lax.all_gather(h_bf, "vp", axis=0, tiled=True)
        labels_all = lax.all_gather(labels, "vp", axis=0, tiled=True)
        mask_all = lax.all_gather(loss_mask, "vp", axis=0, tiled=True)
        vocab_local = w_blk.shape[1]
        col_start = lax.axis_index("vp") * vocab_local
        logits = jnp.einsum("sbd,dv->sbv", h_all, w_blk, preferred_element_type=jnp.float32)
        row_max = lax.pmax(jnp.max(logits, axis=-1), "vp")
        exp_shift = jnp.exp(logits - row_max[:, :, None])
        col_ids = col_start + lax.broadcasted_iota(jnp.int32, (1, 1, vocab_local), 2)
        is_label = col_ids == labels_all[:, :, None]
        sum_exp = lax.psum(jnp.sum(exp_shift, axis=-1), "vp")
        target = lax.psum(jnp.sum(jnp.where(is_label, logits, 0.0), axis=-1), "vp")
        mask_total = jnp.sum(mask_all)
        tok_loss = row_max + jnp.log(sum_exp) - target
        loss = jnp.sum(mask_all * tok_loss) / mask_total
        prob_soft = exp_shift / sum_exp[:, :, None]
        tok_weight = mask_all / mask_total
        grad_logits = (jnp.where(is_label, prob_soft - 1.0, prob_soft) * tok_weight[:, :, None]).astype(jnp.bfloat16)
        grad_w = jnp.einsum("sbd,sbv->dv", h_all, grad_logits, preferred_element_type=jnp.float32)
        grad_h_part = jnp.einsum("sbv,dv->sbd", grad_logits, w_blk, preferred_element_type=jnp.float32)
        grad_h = lax.psum_scatter(grad_h_part, "vp", scatter_dimension=0, tiled=True)
        grad_gain = lax.psum(jnp.sum(grad_h * normed, axis=(0, 1)), "vp")
        grad_bias = lax.psum(jnp.sum(grad_h, axis=(0, 1)), "vp")
        grad_x = norm_backward(grad_h, normed, inv_std, norm_gain)
        return loss.reshape(1), grad_x, grad_w, grad_gain, grad_bias

    tok_spec = P("vp", "dp")
    return jax.shard_map(
        per_device,
        mesh=mesh,
        in_specs=(P("vp", "dp", None), P(None), P(None), P(None, "vp"), tok_spec, tok_spec),
        out_specs=(P("dp"), P("vp", "dp", None), P("dp", "vp"), P("dp"), P("dp")),
        check_vma=False,
    )
```

profile of v0, /device:TPU:0, one launch (start us, length us, event | category | flops | bytes accessed | tf_op | source)
XLA Modules:
  0.0 1216.3 jit_solution(11711882594599612649)
XLA Ops:
  7.2 0.0 all-gather.2.cloned.1.call-start
  7.2 0.7 broadcast_add_fusion
  7.9 0.0 copy-start.2
  7.9 6.6 convert_reduce_fusion
  14.5 0.0 copy-start
  14.5 6.6 fusion.21
  21.2 0.0 copy-done.2
  21.2 0.0 copy-done
  21.2 0.0 copy-start.4
  21.2 0.6 copy-done.4
  21.8 6.5 fusion.15
  28.3 0.0 all-gather.2.cloned.1.call-update
  28.3 0.0 reduce-scatter.2.cloned.1.call-start
  28.4 13.9 %all_gather.9 = f32[128,32]{1,0:T(8,128)S(1)} all-gather(f32[16,32]{1,0:T(8,128)} %param.11), channel_id=1, replica_groups=mesh['dp'=1,'vp'=8] {'vp'}, dimensions={0}, use_global_device_ids=true | all-gather | bytes 18432 | tf_op jit(solution)/shard_map/all_gather | solution.py:30
  42.2 0.1 copy.28
  42.3 0.0 copy-start.14
  42.3 12.0 all_gather.11
  54.3 0.7 copy.27
  55.0 0.6 reduce_sum.95
  55.6 0.6 iota_add_fusion
  56.2 1.3 broadcast_divide_fusion
  57.5 129.8 %all-gather.2.cloned.1.call-done = bf16[128,32,4096]{2,0,1:T(8,128)(2,1)} async-done(((bf16[16,32,4096]{2,0,1:T(8,128)(2,1)}), bf16[128,32,4096]{2,0,1:T(8,128)(2,1)}) %all-gather.2.cloned.1.call-update) | async-done | bytes 33554448 | tf_op jit(solution)/shard_map/all_gather | solution.py:28
  187.3 0.0 copy-start.8
  187.3 0.0 copy-start.10
  187.3 232.1 %fusion.24 = (f32[128,32]{0,1:T(8,128)S(1)}, f32[128,32,6400]{2,0,1:T(8,128)}) fusion(bf16[128,32,4096]{2,0,1:T(8,128)(2,1)} %all-gather.2.cloned.1.call-done, bf16[4096,6400]{1,0:T(8,128)(2,1)} %param.9), kind=kOutput, calls=%fused_computation.37 | convolution fusion | flops 214774579200 | bytes 190857216 | tf_op jit(solution)/shard_map/sbd,dv->sbv/dot_general | solution.py:33
  419.4 0.0 copy-done.14
  419.4 22.3 %pmax.7 = f32[128,32]{0,1:T(8,128)S(1)} all-reduce(f32[128,32]{0,1:T(8,128)S(1)} %get-tuple-element.34), channel_id=1, replica_groups=mesh['dp'=1,'vp'=8] {'vp'}, use_global_device_ids=true, to_apply=%region_3.0 | all-reduce | flops 4096 | bytes 32768 | tf_op jit(solution)/shard_map/pmax | solution.py:34
  441.7 0.0 copy-start.6
  441.7 0.0 copy-done.8
  441.7 0.0 copy-done.10
  441.7 0.0 copy-start.17
  441.7 33.4 %fusion.3 = (f32[128,32]{0,1:T(8,128)S(1)}, f32[128,32]{0,1:T(8,128)}) fusion(f32[128,32,6400]{2,0,1:T(8,128)} %get-tuple-element.35, f32[128,32]{0,1:T(8,128)S(1)} %pmax.7, s32[128,32]{0,1:T(8,128)S(1)} %copy-done.10, s32[6400]{0:T(1024)S(1)} %copy-done.8), kind=kLoop, calls=%fused_computation.6 | loop fusion | flops 131063808 | bytes 104948736 | tf_op jit(solution)/shard_map/reduce_sum | solution.py:38
  475.2 24.1 %psum.28 = f32[128,32]{0,1:T(8,128)S(1)} all-reduce(f32[128,32]{0,1:T(8,128)S(1)} %get-tuple-element.25), channel_id=1, replica_groups=mesh['dp'=1,'vp'=8] {'vp'}, use_global_device_ids=true, to_apply=%region_5.0 | all-reduce | flops 4096 | bytes 32768 | tf_op jit(solution)/shard_map/psum | solution.py:38
  499.2 0.0 copy-done.6
  499.2 0.0 copy-done.17
  499.2 0.0 copy-start.12
  499.2 51.3 %fusion.33 = bf16[128,32,6400]{2,0,1:T(8,128)(2,1)} fusion(f32[128,32,6400]{2,0,1:T(8,128)} %get-tuple-element.35, f32[128,32]{0,1:T(8,128)S(1)} %copy-done.17, f32[128,32]{0,1:T(8,128)S(1)} %psum.28, s32[128,32]{0,1:T(8,128)S(1)} %copy-done.10, s32[6400]{0:T(1024)S(1)} %copy-done.8, f32[128,32]{0,1:T(8,128)S(1)} %pmax.7), kind=kLoop, calls=%fused_computation.4.clone.1.clone.1 | loop fusion | flops 183500800 | bytes 157377536 | tf_op jit(solution)/shard_map/sbv,dv->sbd/dot_general | solution.py:47
  550.5 0.0 copy-done.12
  550.5 233.4 %fusion.4 = f32[128,32,4096]{2,0,1:T(8,128)} fusion(bf16[4096,6400]{1,0:T(8,128)(2,1)} %param.9, bf16[128,32,6400]{2,0,1:T(8,128)(2,1)} %fusion.33), kind=kOutput, calls=%fused_computation.8 | convolution fusion | flops 214748364800 | bytes 171966464 | tf_op jit(solution)/shard_map/sbv,dv->sbd/dot_general | solution.py:47
  783.8 0.0 copy-start.7
  783.8 0.0 copy-start.9
  783.8 0.0 copy-start.13
  783.9 0.0 copy-start.18
  783.9 0.0 reduce-scatter.2.cloned.1.call-update
  783.9 0.7 copy-done.7
  784.6 0.0 copy-done.9
  784.6 0.0 copy-done.11
  784.6 0.0 copy-done.13
  784.6 0.0 copy-done.18
  784.6 0.0 copy-start.5
  784.6 0.0 copy-start.16
  784.7 0.0 copy-start.15
  784.7 282.1 %convolution_bitcast_fusion = f32[4096,6400]{1,0:T(8,128)} fusion(bf16[128,32,4096]{2,0,1:T(8,128)(2,1)} %all-gather.2.cloned.1.call-done, f32[128,32,6400]{2,0,1:T(8,128)} %get-tuple-element.35, f32[128,32]{0,1:T(8,128)S(1)} %copy-done.18, f32[128,32]{0,1:T(8,128)S(1)} %copy-done.13, s32[128,32]{0,1:T(8,128)S(1)} %copy-done.11, s32[6400]{0:T(1024)S(1)} %copy-done.9, ...), kind=kOutput, calls=%fused_computation.7 | convolution fusion | flops 214931865600 | bytes 243360768 | tf_op jit(solution)/shard_map/sbd,sbv->dv/dot_general | solution.py:46
  1066.8 92.9 %reduce-scatter.2.cloned.1.call-done = f32[16,32,4096]{2,0,1:T(8,128)} async-done(((f32[128,32,4096]{2,0,1:T(8,128)}), f32[16,32,4096]{2,0,1:T(8,128)}) %reduce-scatter.2.cloned.1.call-update) | async-done | bytes 8388624 | tf_op jit(solution)/shard_map/reduce_scatter | solution.py:48
  1159.6 0.0 copy-done.1
  1159.6 0.0 copy-done.3
  1159.6 0.0 copy-done.5
  1159.6 11.1 fusion.20
  1170.8 0.0 copy-done.16
  1170.8 23.5 %all-reduce = (f32[128,32]{0,1:T(8,128)S(1)}, f32[4096]{0:T(1024)}, f32[4096]{0:T(1024)}) all-reduce(f32[128,32]{0,1:T(8,128)S(1)} %copy-done.16, f32[4096]{0:T(1024)S(1)} %get-tuple-element.27, f32[4096]{0:T(1024)S(1)} %get-tuple-element.30), channel_id=1, replica_groups=mesh['dp'=1,'vp'=8] {'vp'}, use_global_device_ids=true, to_apply=%region_7.8 | all-reduce | flops 12288 | bytes 98304 | tf_op jit(solution)/shard_map/psum | solution.py:39
  1194.3 0.0 copy-done.15
  1194.3 0.6 multiply_reduce_fusion.1
  1196.3 7.3 fusion.19
  1203.6 4.3 copy.30
  (6 shorter events, 0.0 us)
Async XLA Ops:
  7.2 180.1 %all-gather.2.cloned.1.call-start = ((), (), s32[]{:S(2)}) async-start(), calls=%async_computation.1 | async-start | bytes 37748736 | tf_op jit(solution)/shard_map/all_gather | solution.py:28
  7.9 13.3 %copy-start.2 = (f32[4096]{0:T(1024)}, f32[4096]{0:T(1024)S(1)}, u32[]{:S(2)}) copy-start(f32[4096]{0:T(1024)S(1)} %broadcast_add_fusion) | copy-start | bytes 49156
  14.5 6.7 copy-start
  21.2 0.6 copy-start.4
  28.3 1131.3 %reduce-scatter.2.cloned.1.call-start = ((), (), s32[]{:S(2)}) async-start(), calls=%async_computation.2 | async-start | bytes 75497472 | tf_op jit(solution)/shard_map/reduce_scatter | solution.py:48
  42.3 377.2 %copy-start.14 = (f32[128,32]{0,1:T(8,128)}, f32[128,32]{0,1:T(8,128)S(1)}, u32[]{:S(2)}) copy-start(f32[128,32]{0,1:T(8,128)S(1)} %copy.28) | copy-start | bytes 49156
  187.3 254.4 %copy-start.8 = (s32[6400]{0:T(1024)S(1)}, s32[6400]{0:T(1024)}, u32[]{:S(2)}) copy-start(s32[6400]{0:T(1024)} %iota_add_fusion) | copy-start | bytes 76804
  187.3 254.4 %copy-start.10 = (s32[128,32]{0,1:T(8,128)S(1)}, s32[128,32]{0,1:T(8,128)}, u32[]{:S(2)}) copy-start(s32[128,32]{0,1:T(8,128)} %copy.27) | copy-start | bytes 49156
  441.7 57.5 %copy-start.6 = (f32[128,32]{0,1:T(8,128)}, f32[128,32]{0,1:T(8,128)S(1)}, u32[]{:S(2)}) copy-start(f32[128,32]{0,1:T(8,128)S(1)} %pmax.7) | copy-start | bytes 49156
  441.7 57.5 %copy-start.17 = (f32[128,32]{0,1:T(8,128)S(1)}, f32[128,32]{0,1:T(8,128)}, u32[]{:S(2)}) copy-start(f32[128,32]{0,1:T(8,128)} %broadcast_divide_fusion) | copy-start | bytes 49156
  499.2 51.3 %copy-start.12 = (f32[128,32]{0,1:T(8,128)}, f32[128,32]{0,1:T(8,128)S(1)}, u32[]{:S(2)}) copy-start(f32[128,32]{0,1:T(8,128)S(1)} %psum.28) | copy-start | bytes 49156
  783.8 0.7 copy-start.7
  783.8 0.8 copy-start.9
  783.8 0.8 copy-start.11
  783.8 0.8 copy-start.13
  783.9 0.8 copy-start.18
  784.6 375.0 %copy-start.1 = (f32[16,32]{0,1:T(8,128)S(1)}, f32[16,32]{0,1:T(8,128)}, u32[]{:S(2)}) copy-start(f32[16,32]{0,1:T(8,128)} %copy-done) | copy-start | bytes 6148
  784.6 375.0 %copy-start.3 = (f32[4096]{0:T(1024)S(1)}, f32[4096]{0:T(1024)}, u32[]{:S(2)}) copy-start(f32[4096]{0:T(1024)} %copy-done.2) | copy-start | bytes 49156
  784.6 375.0 %copy-start.5 = (f32[16,32]{0,1:T(8,128)S(1)}, f32[16,32]{0,1:T(8,128)}, u32[]{:S(2)}) copy-start(f32[16,32]{0,1:T(8,128)} %copy-done.4) | copy-start | bytes 6148
  784.6 386.1 %copy-start.16 = (f32[128,32]{0,1:T(8,128)S(1)}, f32[128,32]{0,1:T(8,128)}, u32[]{:S(2)}) copy-start(f32[128,32]{0,1:T(8,128)} %get-tuple-element.26) | copy-start | bytes 49156
  784.7 409.7 %copy-start.15 = (f32[128,32]{0,1:T(8,128)S(1)}, f32[128,32]{0,1:T(8,128)}, u32[]{:S(2)}) copy-start(f32[128,32]{0,1:T(8,128)} %copy-done.14) | copy-start | bytes 49156
Sparse Core Ops, SparseCore 0:
  28.4 158.8 all-gather.1
  784.0 375.5 reduce-scatter.1
where the time goes:
time: 1230 us; the launch traced here: 1220 us
  matrix products  748 us (61%)
  waiting for transfers between devices  223 us (18%)
  other arithmetic  127 us (10%)
  blocking collectives  95.7 us (8%)
  between operations  17.1 us (1%)
    dot_general x1, matrix products, per_device(): jnp.einsum('sbd,sbv->dv', h_all, grad_logits, preferred_element_type=jnp....  282 us
    dot_general x1, matrix products, per_device(): jnp.einsum('sbv,dv->sbd', grad_logits, w_blk, preferred_element_type=jnp....  233 us
    dot_general x1, matrix products, per_device(): jnp.einsum('sbd,dv->sbv', h_all, w_blk, preferred_element_type=jnp.float32)  232 us
    all_gather x1, waiting for transfers between devices, per_device(): h_all = lax.all_gather(h_bf, 'vp', axis=0, tiled=True)  130 us
    reduce_scatter x1, waiting for transfers between devices, per_device(): lax.psum_scatter(grad_h_part, 'vp', scatter_dimension=0, tiled=True)  92.9 us
    dot_general x1, other arithmetic, per_device(): jnp.einsum('sbv,dv->sbd', grad_logits, w_blk, preferred_element_type=jnp....  51.3 us
    reduce_sum x1, other arithmetic, per_device(): sum_exp = lax.psum(jnp.sum(exp_shift, axis=-1), 'vp')  33.4 us
  transfers between devices with their start and end apart: 2, of which 2 were waited for; matrix products, arithmetic and copies ran while one was open for 23% of the time, Pallas kernels for 0%

commit v1 on v0

v1 whole, which is shorter than its diff:
```python
import functools

import jax
import jax.numpy as jnp
from jax import lax
from jax.experimental import pallas as pl
from jax.experimental.pallas import tpu as pltpu
from jax.sharding import PartitionSpec as P

NORM_EPS = 1e-5
MESH = pl.DeviceIdType.MESH
F32, BF16 = jnp.float32, jnp.bfloat16
VMEM_CAP = 66_000_000
STRIP = 64


def norm_kernel(x_ref, g_ref, c_ref, h_ref):
    x = x_ref[...].astype(F32)
    cen = x - jnp.mean(x, axis=-1, keepdims=True)
    inv = lax.rsqrt(jnp.mean(cen * cen, axis=-1, keepdims=True) + NORM_EPS)
    h_ref[...] = (cen * inv * (1.0 + g_ref[...]) + c_ref[...]).astype(BF16)


def norm_fwd(x, g, c):
    rows, d = x.shape
    bm = 128
    vec = pl.BlockSpec((1, d), lambda i: (0, 0))
    return pl.pallas_call(
        norm_kernel,
        grid=(rows // bm,),
        in_specs=[pl.BlockSpec((bm, d), lambda i: (i, 0)), vec, vec],
        out_specs=pl.BlockSpec((bm, d), lambda i: (i, 0)),
        out_shape=jax.ShapeDtypeStruct((rows, d), BF16),
        compiler_params=pltpu.CompilerParams(vmem_limit_bytes=VMEM_CAP),
        name="norm_fwd",
    )(x, g, c)


def logits_kernel(nv, h_ref, w_ref, z_ref, m_ref, s_ref, mx, sm):
    v = pl.program_id(1)
    bm, bn = z_ref.shape
    cut = 256

    @pl.when(v == 0)
    def _():
        mx[...] = jnp.full_like(mx, -jnp.inf)
        sm[...] = jnp.zeros_like(sm)

    for p in range(bn // cut):
        part = slice(cut * p, cut * (p + 1))
        z_ref[:, part] = jnp.dot(h_ref[...], w_ref[:, part], preferred_element_type=F32)
        for r in range(0, bm, STRIP):
            rows = slice(r, r + STRIP)
            zs = [z_ref[rows, c : c + 128] for c in range(cut * p, cut * (p + 1), 128)]
            old = mx[rows]
            new = functools.reduce(jnp.maximum, zs, old)
            acc = sm[rows] * jnp.exp(old - new)
            for z in zs:
                acc = acc + jnp.exp(z - new)
            mx[rows] = new
            sm[rows] = acc

    @pl.when(v == nv - 1)
    def _():
        new = mx[...]
        row_m = jnp.max(new, axis=1, keepdims=True)
        row_s = jnp.sum(sm[...] * jnp.exp(new - row_m), axis=1, keepdims=True)
        for j in range(bm // 128):
            part = slice(128 * j, 128 * (j + 1))
            m_ref[j : j + 1, :] = jnp.broadcast_to(row_m[part], (128, 128)).T[:1]
            s_ref[j : j + 1, :] = jnp.broadcast_to(row_s[part], (128, 128)).T[:1]


def logits_fwd(h, w):
    t, d = h.shape
    vl = w.shape[1]
    bm, bn = 1024, 1280
    stat = pl.BlockSpec((bm // 128, 128), lambda i, v: (i, 0))
    stat_shape = jax.ShapeDtypeStruct((t // 128, 128), F32)
    return pl.pallas_call(
        functools.partial(logits_kernel, vl // bn),
        grid=(t // bm, vl // bn),
        in_specs=[pl.BlockSpec((bm, d), lambda i, v: (i, 0)), pl.BlockSpec((d, bn), lambda i, v: (0, v))],
        out_specs=[pl.BlockSpec((bm, bn), lambda i, v: (i, v)), stat, stat],
        out_shape=[jax.ShapeDtypeStruct((t, vl), F32), stat_shape, stat_shape],
        scratch_shapes=[pltpu.VMEM((bm, 128), F32), pltpu.VMEM((bm, 128), F32)],
        compiler_params=pltpu.CompilerParams(vmem_limit_bytes=VMEM_CAP),
        cost_estimate=pl.CostEstimate(flops=2 * t * d * vl, bytes_accessed=4 * t * vl, transcendentals=0),
        name="logits_fwd",
    )(h, w)


def exchange_kernel(n, post, n_out, x_ref, *rest):
    outs, (recv, send_sem, recv_sem) = rest[:n_out], rest[n_out:]
    me = lax.axis_index("vp")
    zero = lax.axis_index("dp")
    barrier = pltpu.get_barrier_semaphore()
    for k in range(1, n):
        pl.semaphore_signal(barrier, inc=1, device_id=(zero, lax.rem(me + k, n)), device_id_type=MESH)
    pl.semaphore_wait(barrier, n - 1)
    copies = []
    for k in range(1, n):
        copy = pltpu.make_async_remote_copy(
            src_ref=x_ref,
            dst_ref=recv.at[me],
            send_sem=send_sem.at[k],
            recv_sem=recv_sem.at[k],
            device_id=(zero, lax.rem(me + k, n)),
            device_id_type=MESH,
        )
        copy.start()
        copies.append(copy)
    recv[me] = x_ref[...]
    for copy in copies:
        copy.wait()
    post([recv[k] for k in range(n)], outs)


def exchange(x, n, post, out_shapes, cid, name):
    return pl.pallas_call(
        functools.partial(exchange_kernel, n, post, len(out_shapes)),
        in_specs=[pl.BlockSpec(memory_space=pltpu.VMEM)],
        out_specs=[pl.BlockSpec(memory_space=pltpu.VMEM)] * len(out_shapes),
        out_shape=out_shapes,
        scratch_shapes=[
            pltpu.VMEM((n,) + x.shape, x.dtype),
            pltpu.SemaphoreType.DMA((n,)),
            pltpu.SemaphoreType.DMA((n,)),
        ],
        compiler_params=pltpu.CompilerParams(collective_id=cid, has_side_effects=True),
        name=name,
    )(x)


def stats_post(rows, own, parts, outs):
    m_ref, a_ref, lab_ref, misc_ref = outs
    top = parts[0][:rows]
    for p in parts[1:]:
        top = jnp.maximum(top, p[:rows])
    tot = parts[0][rows : 2 * rows] * jnp.exp(parts[0][:rows] - top)
    for p in parts[1:]:
        tot = tot + p[rows : 2 * rows] * jnp.exp(p[:rows] - top)
    lab = jnp.concatenate([p[2 * rows : 2 * rows + own] for p in parts], axis=0)
    mask = jnp.where(lab >= 0.0, 1.0, 0.0)
    count = jnp.sum(mask)
    m_ref[...] = top
    a_ref[...] = mask / count / tot
    lab_ref[...] = lab
    misc_ref[0:8, :] = jnp.full((8, 128), 1.0, F32) / count
    misc_ref[8:16, :] = jnp.full((8, 128), jnp.sum(mask * (top + jnp.log(tot))), F32)


def grad_h_kernel(nk, nn, z_ref, m_ref, a_ref, lab_ref, inv_ref, w_ref, *rest):
    dh_ref, dz_ref, t_ref, dz_s = rest[-4:]
    i = pl.program_id(0)
    groups, _, rows, bk = z_ref.shape
    bn = w_ref.shape[0]
    cut = 256
    contract = (((1,), (1,)), ((), ()))

    def make_dz():
        inv = jnp.broadcast_to(inv_ref[0:1, :], (STRIP, 128))
        lane = lax.broadcasted_iota(jnp.int32, (STRIP, 128), 1)
        hit_sum = jnp.zeros((STRIP, 128), F32)
        lanes = [(lane + (i * bk + 128 * j)).astype(F32) for j in range(bk // 128)]
        for grp in range(groups):
            for r in range(0, rows, STRIP):
                part = slice(r, r + STRIP)
                m, a, lab = m_ref[grp, 0, part], a_ref[grp, 0, part], lab_ref[grp, 0, part]
                for j in range(bk // 128):
                    cols = slice(128 * j, 128 * (j + 1))
                    z = z_ref[grp, 0, part, cols]
                    hit = lab == lanes[j]
                    hit_sum = hit_sum + jnp.where(hit, z, 0.0)
                    dz = (jnp.exp(z - m) * a - jnp.where(hit, inv, 0.0)).astype(BF16)
                    dz_s[i, grp * rows + r : grp * rows + r + STRIP, cols] = dz
                    dz_ref[grp, 0, part, cols] = dz
        for r in range(0, STRIP, 8):
            t_ref[...] += hit_sum[r : r + 8]

    def product():
        k = lax.rem(i - 1, nk)
        keep = jnp.where(k == 0, 0.0, 1.0)
        for p in range(bn // cut):
            part = lax.dot_general(
                dz_s[k], w_ref[cut * p : cut * (p + 1), :], contract, preferred_element_type=F32
            )
            cols = slice(cut * p, cut * (p + 1))
            dh_ref[:, cols] = jnp.where(k == 0, 0.0, dh_ref[:, cols]) + part

    @pl.when(i == 0)
    def _():
        t_ref[...] = jnp.zeros_like(t_ref)
        make_dz()

    @pl.when((i > 0) & (i < nk))
    def _():
        product()
        make_dz()

    @pl.when(i >= nk)
    def _():
        product()


def grad_h_chunk(z4, m4, a4, lab4, inv, w, dz4, c):
    groups, _, rows, vl = z4.shape
    d = w.shape[0]
    bn, bk = 1024, 1280
    nk, nn = vl // bk, d // bn
    t = groups * rows
    tile = pl.BlockSpec((groups, 1, rows, bk), lambda i: (0, c, 0, jnp.minimum(i, nk - 1)))
    col = pl.BlockSpec((groups, 1, rows, 128), lambda i: (0, c, 0, 0))
    small = pl.BlockSpec((8, 128), lambda i: (0, 0))
    in_specs = [tile, col, col, col, small, pl.BlockSpec((bn, bk), lambda i: (jnp.maximum(i - 1, 0) // nk, lax.rem(jnp.maximum(i - 1, 0), nk)))]
    args = [z4, m4, a4, lab4, inv, w]
    aliases = {}
    if dz4 is not None:
        in_specs.append(pl.BlockSpec(memory_space=pl.ANY))
        aliases = {len(args): 1}
        args.append(dz4)
    return pl.pallas_call(
        functools.partial(grad_h_kernel, nk, nn),
        grid=(nk * nn + 1,),
        in_specs=in_specs,
        out_specs=[pl.BlockSpec((t, bn), lambda i: (0, jnp.maximum(i - 1, 0) // nk)), tile, small],
        out_shape=[
            jax.ShapeDtypeStruct((t, d), F32),
            jax.ShapeDtypeStruct(z4.shape, BF16),
            jax.ShapeDtypeStruct((8, 128), F32),
        ],
        scratch_shapes=[pltpu.VMEM((nk, t, bk), BF16)],
        input_output_aliases=aliases,
        compiler_params=pltpu.CompilerParams(vmem_limit_bytes=VMEM_CAP),
        cost_estimate=pl.CostEstimate(flops=2 * t * d * vl, bytes_accessed=4 * t * vl, transcendentals=0),
        name="grad_h",
    )(*args)


def grad_w_kernel(h_ref, dz_ref, out_ref):
    out_ref[...] = lax.dot_general(h_ref[...], dz_ref[...], (((0,), (0,)), ((), ())), preferred_element_type=F32)


def grad_w_call(h, dz):
    t, d = h.shape
    vl = dz.shape[1]
    bm, bn = 1024, 1280
    return pl.pallas_call(
        grad_w_kernel,
        grid=(vl // bn, d // bm),
        in_specs=[pl.BlockSpec((t, bm), lambda v, i: (0, i)), pl.BlockSpec((t, bn), lambda v, i: (0, v))],
        out_specs=pl.BlockSpec((bm, bn), lambda v, i: (i, v)),
        out_shape=jax.ShapeDtypeStruct((d, vl), F32),
        compiler_params=pltpu.CompilerParams(vmem_limit_bytes=VMEM_CAP),
        cost_estimate=pl.CostEstimate(flops=2 * t * d * vl, bytes_accessed=4 * d * vl, transcendentals=0),
        name="grad_w",
    )(h, dz)


def norm_bwd_kernel(nc, x_ref, g_ref, *rest):
    dh_refs, dx_ref, sums_ref = rest[:nc], rest[nc], rest[nc + 1]
    rows, d = dh_refs[0].shape
    gain = 1.0 + g_ref[...]
    step = 32
    for c in range(nc):
        def body(i, sums, c=c):
            part = pl.ds(pl.multiple_of(i * step, step), step)
            x = x_ref[pl.ds(pl.multiple_of(c * rows + i * step, step), step), :].astype(F32)
            dh = dh_refs[c][part, :]
            cen = x - jnp.mean(x, axis=-1, keepdims=True)
            inv = lax.rsqrt(jnp.mean(cen * cen, axis=-1, keepdims=True) + NORM_EPS)
            nrm = cen * inv
            q = dh * gain
            q_mean = jnp.mean(q, axis=-1, keepdims=True)
            qn_mean = jnp.mean(q * nrm, axis=-1, keepdims=True)
            dx = inv * (q - q_mean - nrm * qn_mean)
            dx_ref[pl.ds(pl.multiple_of(c * rows + i * step, step), step), :] = dx.astype(BF16)
            sums_ref[0:8, :] += jnp.sum((dh * nrm).reshape(step // 8, 8, d), axis=0)
            sums_ref[8:16, :] += jnp.sum(dh.reshape(step // 8, 8, d), axis=0)
            return sums
        if c == 0:
            sums_ref[...] = jnp.zeros_like(sums_ref)
        lax.fori_loop(0, rows // step, body, 0)


def norm_bwd(x, g, dhs):
    rows, d = x.shape
    vm = pl.BlockSpec(memory_space=pltpu.VMEM)
    return pl.pallas_call(
        functools.partial(norm_bwd_kernel, len(dhs)),
        in_specs=[vm] * (2 + len(dhs)),
        out_specs=[vm, vm],
        out_shape=[jax.ShapeDtypeStruct((rows, d), BF16), jax.ShapeDtypeStruct((16, d), F32)],
        compiler_params=pltpu.CompilerParams(vmem_limit_bytes=VMEM_CAP),
        name="norm_bwd",
    )(x, g, *dhs)


def final_post(rows, parts, outs):
    tot = parts[0]
    for p in parts[1:]:
        tot = tot + p
    outs[0][...] = tot[:rows]
    outs[1][...] = jnp.full((8, 128), jnp.sum(tot[rows : rows + 8]), F32)


def solution(mesh):
    n = mesh.shape["vp"]

    def per_device(hidden, norm_gain, norm_bias, w, labels, loss_mask):
        s_loc, b_loc, d = hidden.shape
        rows = s_loc * b_loc
        t = rows * n
        vl = w.shape[1]
        nc = rows // 128
        x = hidden.reshape(rows, d)
        g = norm_gain.reshape(1, d)
        h_own = norm_fwd(x, g, norm_bias.reshape(1, d))
        h = lax.all_gather(h_own, "vp", axis=0, tiled=True)
        z, m_loc, s_loc_sum = logits_fwd(h, w)

        lab_own = jnp.where(loss_mask > 0.0, labels, -1).astype(F32).reshape(nc, 128)
        stat_rows = t // 128
        packed = jnp.concatenate([m_loc, s_loc_sum, lab_own, jnp.zeros((8 - nc % 8, 128), F32)], axis=0)
        compact = jax.ShapeDtypeStruct((stat_rows, 128), F32)
        m, a, lab, misc = exchange(
            packed,
            n,
            functools.partial(stats_post, stat_rows, nc),
            [compact, compact, compact, jax.ShapeDtypeStruct((16, 128), F32)],
            0,
            "stats_exchange",
        )
        col_start = (lax.axis_index("vp") * vl).astype(F32)

        def wide(v):
            return jnp.broadcast_to(v[:, :, None], (stat_rows, 128, 128)).reshape(n, nc, 128, 128)

        m4, a4, lab4 = wide(m), wide(a), wide(lab - col_start)
        z4 = z.reshape(n, nc, 128, vl)
        inv = misc[:8]
        dz4, dhs, hits = None, [], []
        for c in range(nc):
            dh_c, dz4, hit = grad_h_chunk(z4, m4, a4, lab4, inv, w, dz4, c)
            hits.append(hit)
            dhs.append(lax.psum_scatter(dh_c, "vp", scatter_dimension=0, tiled=True))
        grad_w = grad_w_call(h, dz4.reshape(t, vl))
        grad_x, sums = norm_bwd(x, g, dhs)
        vecs = jnp.sum(sums.reshape(2, 8, d), axis=1).reshape(2 * d // 128, 128)
        packed2 = jnp.concatenate([vecs, sum(hits)], axis=0)
        vrows = 2 * d // 128
        out_vec, hit_tot = exchange(
            packed2,
            n,
            functools.partial(final_post, vrows),
            [jax.ShapeDtypeStruct((vrows, 128), F32), jax.ShapeDtypeStruct((8, 128), F32)],
            1,
            "final_exchange",
        )
        loss = (misc[8, 0] - hit_tot[0, 0]) * misc[0, 0]
        out_vec = out_vec.reshape(2, d)
        return loss.reshape(1), grad_x.reshape(hidden.shape), grad_w, out_vec[0], out_vec[1]

    tok_spec = P("vp", "dp")
    return jax.shard_map(
        per_device,
        mesh=mesh,
        in_specs=(P("vp", "dp", None), P(None), P(None), P(None, "vp"), tok_spec, tok_spec),
        out_specs=(P("dp"), P("vp", "dp", None), P("dp", "vp"), P("dp"), P("dp")),
        check_vma=False,
    )
```

time: 1230 us -> 1020 us (0.83)
  Pallas kernels: 0 us -> 817 us
  matrix products: 748 us -> 0 us
  other arithmetic: 127 us -> 5.12 us
  blocking collectives: 95.7 us -> 0 us
  waiting for transfers between devices: 223 us -> 157 us
    pallas_call x0 -> x10, Pallas kernels: none -> 817 us  [the longest x4 308 us: grad_h_chunk(): pl.pallas_call(functools.partial(grad_h_kernel, nk, nn), grid=(nk * nn +...]
    dot_general x3 -> x0, matrix products: 748 us -> none  [the longest x1 282 us: per_device(): jnp.einsum('sbd,sbv->dv', h_all, grad_logits, preferred_element_type=jnp....]
    reduce_scatter x1 -> x4, waiting for transfers between devices: 92.9 us -> 0.03 us  [per_device(): dhs.append(lax.psum_scatter(dh_c, 'vp', scatter_dimension=0, tiled=True))]
    reduce_sum x6 -> x1, other arithmetic: 59 us -> 1.03 us  [per_device(): vecs = jnp.sum(sums.reshape(2, 8, d), axis=1).reshape(2 * d // 128, 128)]
    dot_general x1 -> x0, other arithmetic: 51.3 us -> none  [per_device(): jnp.einsum('sbv,dv->sbd', grad_logits, w_blk, preferred_element_type=jnp....]
    psum x2 -> x0, blocking collectives: 47.6 us -> none  [the longest x1 24.1 us: per_device(): sum_exp = lax.psum(jnp.sum(exp_shift, axis=-1), 'vp')]
    all_gather x1, waiting for transfers between devices: 130 us -> 156 us  [per_device(): h = lax.all_gather(h_own, 'vp', axis=0, tiled=True)]
    all_gather x2 -> x0, blocking collectives: 25.9 us -> none  [the longest x1 13.9 us: per_device(): mask_all = lax.all_gather(loss_mask, 'vp', axis=0, tiled=True)]
  transfers between devices with their start and end apart: 2 -> 5, of which waited for: 2 -> 1; matrix products, arithmetic and copies ran while one was open for 23% -> 0% of each run, Pallas kernels for 0% -> 46%
where the time goes in v1:
time: 1020 us; the launch traced here: 1010 us
  Pallas kernels  817 us (80%)
  waiting for transfers between devices  157 us (15%)
  between operations  17.4 us (2%)
  local copies, waits for them, and re-layouts  13.7 us (1%)
    pallas_call x4, Pallas kernels, grad_h_chunk(): pl.pallas_call(functools.partial(grad_h_kernel, nk, nn), grid=(nk * nn +...  308 us
    pallas_call x1, Pallas kernels, logits_fwd(): pl.pallas_call(functools.partial(logits_kernel, vl // bn), grid=(t // bm,...  237 us
    pallas_call x1, Pallas kernels, grad_w_call(): pl.pallas_call(grad_w_kernel, grid=(vl // bn, d // bm), in_specs=[pl.Bloc...  233 us
    all_gather x1, waiting for transfers between devices, per_device(): h = lax.all_gather(h_own, 'vp', axis=0, tiled=True)  156 us
  transfers between devices with their start and end apart: 5, of which 1 were waited for; matrix products, arithmetic and copies ran while one was open for 0% of the time, Pallas kernels for 46%

profile of v1, /device:TPU:0, one launch (start us, length us, event | category | flops | bytes accessed | tf_op | source)
XLA Modules:
  0.0 1010.4 jit_solution(18021545763615319386)
XLA Ops:
  7.2 0.0 all-gather.2.cloned.1.call-start
  7.2 7.0 norm_fwd.1
  14.3 0.0 all-gather.2.cloned.1.call-update
  14.3 0.0 reduce-scatter.5.cloned.1.call-start
  14.3 0.7 select_convert_fusion
  15.1 0.7 reshape.63
  15.7 0.6 pad.5.clone
  16.3 156.2 %all-gather.2.cloned.1.call-done.h_ref = bf16[4096,4096]{1,0:T(8,128)(2,1)} async-done(((bf16[512,4096]{1,0:T(8,128)(2,1)}), bf16[4096,4096]{1,0:T(8,128)(2,1)}) %all-gather.2.cloned.1.call-update) | async-done | bytes 33554448 | tf_op jit(solution)/shard_map/all_gather | solution.py:319
  172.5 0.0 copy-start.1
  172.5 0.0 copy-start.6
  172.5 237.2 %logits_fwd.1 = (f32[4096,6400]{1,0:T(8,128)}, f32[32,128]{1,0:T(8,128)}, f32[32,128]{1,0:T(8,128)}) custom-call(bf16[4096,4096]{1,0:T(8,128)(2,1)} %all-gather.2.cloned.1.call-done.h_ref, bf16[4096,6400]{1,0:T(8,128)(2,1)} %w_ref.9), custom_call_target="tpu_custom_call" | custom-call | flops 214748364800 | bytes 104857600 | tf_op jit(solution)/shard_map/logits_fwd/pallas_call | solution.py:80
  409.7 0.0 copy-done.1
  409.7 0.0 copy-done.6
  409.7 1.4 maximum_maximum_fusion.x_ref
  411.2 8.0 stats_exchange.1
  419.2 1.3 slice.21.inv_ref
  420.5 0.7 broadcast_subtract_fusion
  421.2 2.0 broadcast_in_dim.38.lab_ref
  423.2 2.7 broadcast_in_dim.36.a_ref
  425.8 2.6 broadcast_in_dim.34.m_ref
  428.5 77.0 %grad_h.4 = (f32[1024,4096]{1,0:T(8,128)}, bf16[8,4,128,6400]{3,2,1,0:T(8,128)(2,1)}, f32[8,128]{1,0:T(8,128)}) custom-call(f32[8,4,128,6400]{3,2,1,0:T(8,128)} %bitcast.3.z_ref, f32[8,4,128,128]{3,2,1,0:T(8,128)} %broadcast_in_dim.34.m_ref, f32[8,4,128,128]{3,2,1,0:T(8,128)} %broadcast_in_dim.36.a_ref, f32[8,4,128,128]{3,2,1,0:T(8,128)} %broadcast_in_dim.38.lab_ref, ...), custom_call_target="tpu_custom_call" | custom-call | flops 53687091200 | bytes 26214400 | tf_op jit(solution)/shard_map/grad_h/pallas_call | solution.py:222
  505.5 0.0 reduce-scatter.5.cloned.1.call-update
  505.5 0.0 reduce-scatter.7.cloned.1.call-start
  505.6 76.9 %grad_h.5 = (f32[1024,4096]{1,0:T(8,128)}, bf16[8,4,128,6400]{3,2,1,0:T(8,128)(2,1)}, f32[8,128]{1,0:T(8,128)}) custom-call(f32[8,4,128,6400]{3,2,1,0:T(8,128)} %bitcast.3.z_ref, f32[8,4,128,128]{3,2,1,0:T(8,128)} %broadcast_in_dim.34.m_ref, f32[8,4,128,128]{3,2,1,0:T(8,128)} %broadcast_in_dim.36.a_ref, ...), custom_call_target="tpu_custom_call", output_to_operand_aliasing={{1}: (6, {})} | custom-call | flops 53687091200 | bytes 26214400 | tf_op jit(solution)/shard_map/grad_h/pallas_call | solution.py:222
  582.4 0.0 reduce-scatter.7.cloned.1.call-update
  582.5 0.0 reduce-scatter.11.cloned.1.call-start
  582.5 76.9 %grad_h.6 = (f32[1024,4096]{1,0:T(8,128)}, bf16[8,4,128,6400]{3,2,1,0:T(8,128)(2,1)}, f32[8,128]{1,0:T(8,128)}) custom-call(f32[8,4,128,6400]{3,2,1,0:T(8,128)} %bitcast.3.z_ref, f32[8,4,128,128]{3,2,1,0:T(8,128)} %broadcast_in_dim.34.m_ref, f32[8,4,128,128]{3,2,1,0:T(8,128)} %broadcast_in_dim.36.a_ref, ...), custom_call_target="tpu_custom_call", output_to_operand_aliasing={{1}: (6, {})} | custom-call | flops 53687091200 | bytes 26214400 | tf_op jit(solution)/shard_map/grad_h/pallas_call | solution.py:222
  659.4 76.9 %grad_h.7 = (f32[1024,4096]{1,0:T(8,128)}, bf16[8,4,128,6400]{3,2,1,0:T(8,128)(2,1)}, f32[8,128]{1,0:T(8,128)}) custom-call(f32[8,4,128,6400]{3,2,1,0:T(8,128)} %bitcast.3.z_ref, f32[8,4,128,128]{3,2,1,0:T(8,128)} %broadcast_in_dim.34.m_ref, f32[8,4,128,128]{3,2,1,0:T(8,128)} %broadcast_in_dim.36.a_ref, ...), custom_call_target="tpu_custom_call", output_to_operand_aliasing={{1}: (6, {})} | custom-call | flops 53687091200 | bytes 26214400 | tf_op jit(solution)/shard_map/grad_h/pallas_call | solution.py:222
  736.3 0.0 copy-start.2
  736.3 0.0 copy-start.3
  736.3 0.0 copy-start.4
  736.3 0.0 copy-start.5
  736.3 0.0 reduce-scatter.11.cloned.1.call-update
  736.4 0.0 reduce-scatter.9.cloned.1.call-start
  736.4 0.5 reduce-scatter.9.cloned.1.call-update
  737.0 1.3 fusion
  738.2 0.0 copy-done.2
  738.2 0.0 copy-done.3
  738.2 0.0 copy-done.4
  738.3 0.0 copy-done.5
  738.3 0.6 add_add_fusion
  738.9 0.0 copy-start
  738.9 233.3 %grad_w.1 = f32[4096,6400]{1,0:T(8,128)} custom-call(bf16[4096,4096]{1,0:T(8,128)(2,1)} %all-gather.2.cloned.1.call-done.h_ref, bf16[4096,6400]{1,0:T(8,128)(2,1)} %bitcast.16), custom_call_target="tpu_custom_call" | custom-call | flops 214748364800 | bytes 104857600 | tf_op jit(solution)/shard_map/grad_w/pallas_call | solution.py:248
  972.1 0.0 reduce-scatter.5.cloned.1.call-done.rest_0_
  972.1 0.0 reduce-scatter.7.cloned.1.call-done.rest_1_
  972.1 0.0 reduce-scatter.11.cloned.1.call-done.rest_3_
  972.1 0.0 reduce-scatter.9.cloned.1.call-done.rest_2_
  972.2 15.6 %norm_bwd.1 = (bf16[512,4096]{1,0:T(8,128)(2,1)}, f32[16,4096]{1,0:T(8,128)}) custom-call(bf16[512,4096]{1,0:T(8,128)(2,1)} %bitcast.18, f32[1,4096]{1,0:T(1,128)} %bitcast.20, f32[128,4096]{1,0:T(8,128)} %reduce-scatter.5.cloned.1.call-done.rest_0_, f32[128,4096]{1,0:T(8,128)} %reduce-scatter.7.cloned.1.call-done.rest_1_, ...), custom_call_target="tpu_custom_call" | custom-call | tf_op jit(solution)/shard_map/norm_bwd/pallas_call | solution.py:289
  987.7 1.0 bitcast_reduce_fusion
  988.8 0.0 copy-done
  988.8 0.6 pad_maximum_fusion.x_ref
  989.5 8.4 final_exchange.1
  997.9 1.2 slice.22
  999.1 1.3 slice_bitcast_fusion
  (2 shorter events, 0.0 us)
Async XLA Ops:
  7.2 165.3 %all-gather.2.cloned.1.call-start = ((), (), s32[]{:S(2)}) async-start(), calls=%async_computation.4 | async-start | bytes 37748736 | tf_op jit(solution)/shard_map/all_gather | solution.py:319
  14.3 957.8 %reduce-scatter.5.cloned.1.call-start = ((), (), s32[]{:S(2)}) async-start(), calls=%async_computation.5 | async-start | bytes 18874368 | tf_op jit(solution)/shard_map/reduce_scatter | solution.py:346
  172.5 237.2 %copy-start.1 = (f32[4,128]{1,0:T(4,128)S(1)}, f32[4,128]{1,0:T(4,128)}, u32[]{:S(2)}) copy-start(f32[4,128]{1,0:T(4,128)} %reshape.63) | copy-start | bytes 6148
  172.5 237.2 %copy-start.6 = (f32[72]{0:T(128)S(1)}, f32[72]{0:T(128)}, u32[]{:S(2)}) copy-start(f32[72]{0:T(128)} %pad.5.clone) | copy-start | bytes 868
  505.5 466.6 %reduce-scatter.7.cloned.1.call-start = ((), (), s32[]{:S(2)}) async-start(), calls=%async_computation.6 | async-start | bytes 18874368 | tf_op jit(solution)/shard_map/reduce_scatter | solution.py:346
  582.5 389.7 %reduce-scatter.11.cloned.1.call-start = ((), (), s32[]{:S(2)}) async-start(), calls=%async_computation.8 | async-start | bytes 18874368 | tf_op jit(solution)/shard_map/reduce_scatter | solution.py:346
  736.3 1.9 copy-start.2
  736.3 1.9 copy-start.3
  736.3 1.9 copy-start.4
  736.3 1.9 copy-start.5
  736.4 235.8 %reduce-scatter.9.cloned.1.call-start = ((), (), s32[]{:S(2)}) async-start(), calls=%async_computation.7 | async-start | bytes 18874368 | tf_op jit(solution)/shard_map/reduce_scatter | solution.py:346
  738.9 250.0 %copy-start = (f32[8,128]{1,0:T(8,128)S(1)}, f32[8,128]{1,0:T(8,128)}, u32[]{:S(2)}) copy-start(f32[8,128]{1,0:T(8,128)} %add_add_fusion) | copy-start | bytes 12292
Sparse Core Ops, SparseCore 0:
  14.4 158.0 all-gather.1
  505.6 107.3 reduce-scatter.4
  616.6 106.9 reduce-scatter.6
  736.5 107.3 reduce-scatter.10
  847.2 106.9 reduce-scatter.8

commit v2 on v1

--- a/solution.py
+++ b/solution.py
@@ -36,22 +36,156 @@
     )(x, g, c)
 
 
-def logits_kernel(nv, h_ref, w_ref, z_ref, m_ref, s_ref, mx, sm):
-    v = pl.program_id(1)
-    bm, bn = z_ref.shape
+def gather_logits_kernel(nv, own_ref, w_ref, all_ref, z_ref, m_ref, s_ref, hbuf, zbuf, mx, sm, send_sem, recv_sem, load_sem, own_sem, z_sem):
+    i = pl.program_id(0)
+    u, v = lax.div(i, nv), lax.rem(i, nv)
+    last = 4 * nv - 1
+    blk = own_ref.shape[0]
+    half = blk // 2
+    bm, bn = zbuf.shape[1:]
     cut = 256
+    zero = lax.axis_index("dp")
+    me = lax.axis_index("vp")
+    core = (zero, me + 1 - 2 * lax.rem(me, 2))
+    over_x = (zero, me + 2 - 4 * lax.rem(lax.div(me, 2), 2))
+    over_y = (zero, me + 4 - 8 * lax.div(me, 4))
+
+    def piece(slot, part):
+        return pl.ds(slot * blk + max(part, 0) * half, blk if part < 0 else half)
+
+    def remote(k, src, dst, to):
+        return pltpu.make_async_remote_copy(
+            src_ref=src,
+            dst_ref=all_ref.at[dst],
+            send_sem=send_sem.at[k],
+            recv_sem=recv_sem.at[k],
+            device_id=to,
+            device_id_type=MESH,
+        )
+
+    def forward(k, slot, part, slot_to, to):
+        return remote(k, all_ref.at[piece(slot, part)], piece(slot_to, part), to)
+
+    copies = [
+        remote(0, own_ref, piece(1, -1), core),
+        remote(1, own_ref.at[piece(0, 0)], piece(2, 0), over_x),
+        remote(2, own_ref.at[piece(0, 0)], piece(4, 0), over_y),
+        remote(3, own_ref.at[piece(0, 1)], piece(2, 1), over_x),
+        remote(4, own_ref.at[piece(0, 1)], piece(4, 1), over_y),
+        forward(5, 2, 0, 3, core),
+        forward(6, 4, 0, 5, core),
+        forward(7, 4, 0, 6, over_x),
+        forward(8, 2, 1, 3, core),
+        forward(9, 4, 1, 5, core),
+        forward(10, 2, 1, 6, over_y),
+        forward(11, 6, -1, 7, core),
+    ]
+
+    def load(src, b, q, count):
+        return pltpu.make_async_copy(src, hbuf.at[b, pl.ds(q * half, count * half)], load_sem.at[b, q])
+
+    def load_slot(slot, part, b, q):
+        return load(all_ref.at[piece(slot, part)], b, q, 2 if part < 0 else 1)
+
+    keep_own = pltpu.make_async_copy(hbuf.at[0, pl.ds(0, blk)], all_ref.at[piece(0, -1)], own_sem)
+
+    @pl.when(i == 0)
+    def _():
+        own_load = load(own_ref, 0, 0, 2)
+        own_load.start()
+        barrier = pltpu.get_barrier_semaphore()
+        for to in (core, over_x, over_y):
+            pl.semaphore_signal(barrier, inc=1, device_id=to, device_id_type=MESH)
+        pl.semaphore_wait(barrier, 3)
+        for k in range(5):
+            copies[k].start()
+        own_load.wait()
+        keep_own.start()
+        copies[0].wait_recv()
+        other = load_slot(1, -1, 0, 2)
+        other.start()
+        other.wait()
+
+    @pl.when(i == nv - 1)
+    def _():
+        keep_own.wait()
+        for k in (1, 2):
+            copies[k].wait_recv()
+        for k in (5, 6, 7):
+            copies[k].start()
+        load_slot(2, 0, 1, 0).start()
+        load_slot(4, 0, 1, 2).start()
+
+    @pl.when(i == nv)
+    def _():
+        for k in (5, 6):
+            copies[k].wait_recv()
+        load_slot(3, 0, 1, 1).start()
+        load_slot(5, 0, 1, 3).start()
+        for q in range(4):
+            load_slot(2 + q, 0, 1, q).wait()
+
+    @pl.when(i == 2 * nv - 2)
+    def _():
+        for k in (3, 4):
+            copies[k].wait_recv()
+        for k in (8, 9, 10):
+            copies[k].start()
+        load_slot(2, 1, 0, 0).start()
+        load_slot(4, 1, 0, 2).start()
+
+    @pl.when(i == 2 * nv)
+    def _():
+        for k in (8, 9):
+            copies[k].wait_recv()
+        load_slot(3, 1, 0, 1).start()
+        load_slot(5, 1, 0, 3).start()
+        for q in range(4):
+            load_slot(2 + q, 1, 0, q).wait()
+
+    @pl.when(i == 3 * nv - 2)
+    def _():
+        for k in (7, 10):
+            copies[k].wait_recv()
+        copies[11].start()
+        load_slot(6, -1, 1, 0).start()
+
+    @pl.when(i == 3 * nv)
+    def _():
+        copies[11].wait_recv()
+        load_slot(7, -1, 1, 2).start()
+        load_slot(6, -1, 1, 0).wait()
+        load_slot(7, -1, 1, 2).wait()
+
+    def row_of(unit, q):
+        edge = (unit == 0) | (unit == 3)
+        return jnp.where(edge, unit * 4 * half + q * half, (4 + 2 * q) * half + (unit - 1) * half)
+
+    def put(step, q):
+        row = pl.multiple_of(row_of(lax.div(step, nv), q), half)
+        col = pl.multiple_of(lax.rem(step, nv) * bn, bn)
+        b = lax.rem(step, 2)
+        return pltpu.make_async_copy(
+            zbuf.at[b, pl.ds(q * half, half)], z_ref.at[pl.ds(row, half), pl.ds(col, bn)], z_sem.at[b, q]
+        )
+
+    @pl.when(i >= 2)
+    def _():
+        for q in range(4):
+            put(i - 2, q).wait()
 
     @pl.when(v == 0)
     def _():
         mx[...] = jnp.full_like(mx, -jnp.inf)
         sm[...] = jnp.zeros_like(sm)
 
+    hb, zb = lax.rem(u, 2), lax.rem(i, 2)
     for p in range(bn // cut):
         part = slice(cut * p, cut * (p + 1))
-        z_ref[:, part] = jnp.dot(h_ref[...], w_ref[:, part], preferred_element_type=F32)
+        zbuf[zb, :, part] = jnp.dot(hbuf[hb], w_ref[:, part], preferred_element_type=F32)
         for r in range(0, bm, STRIP):
             rows = slice(r, r + STRIP)
-            zs = [z_ref[rows, c : c + 128] for c in range(cut * p, cut * (p + 1), 128)]
+            zs = [zbuf[zb, rows, c : c + 128] for c in range(cut * p, cut * (p + 1), 128)]
             old = mx[rows]
             new = functools.reduce(jnp.maximum, zs, old)
             acc = sm[rows] * jnp.exp(old - new)
@@ -60,34 +194,62 @@
             mx[rows] = new
             sm[rows] = acc
 
+    for q in range(4):
+        put(i, q).start()
+
     @pl.when(v == nv - 1)
     def _():
         new = mx[...]
         row_m = jnp.max(new, axis=1, keepdims=True)
         row_s = jnp.sum(sm[...] * jnp.exp(new - row_m), axis=1, keepdims=True)
+        per = half // 128
         for j in range(bm // 128):
             part = slice(128 * j, 128 * (j + 1))
-            m_ref[j : j + 1, :] = jnp.broadcast_to(row_m[part], (128, 128)).T[:1]
-            s_ref[j : j + 1, :] = jnp.broadcast_to(row_s[part], (128, 128)).T[:1]
-
-
-def logits_fwd(h, w):
-    t, d = h.shape
+            row = lax.div(row_of(u, j // per), 128) + j % per
+            m_ref[pl.ds(row, 1), :] = jnp.broadcast_to(row_m[part], (128, 128)).T[:1]
+            s_ref[pl.ds(row, 1), :] = jnp.broadcast_to(row_s[part], (128, 128)).T[:1]
+
+    @pl.when(i == last)
+    def _():
+        for k in range(12):
+            copies[k].wait_send()
+        for q in range(4):
+            put(i - 1, q).wait()
+            put(i, q).wait()
+
+
+def gather_logits(h_own, w, n):
+    blk, d = h_own.shape
+    t = n * blk
     vl = w.shape[1]
-    bm, bn = 1024, 1280
-    stat = pl.BlockSpec((bm // 128, 128), lambda i, v: (i, 0))
+    bm, bn = 2 * blk, 1280
+    nv = vl // bn
+    stat = pl.BlockSpec((t // 128, 128), lambda i: (0, 0))
     stat_shape = jax.ShapeDtypeStruct((t // 128, 128), F32)
+    hbm = pl.BlockSpec(memory_space=pl.ANY)
     return pl.pallas_call(
-        functools.partial(logits_kernel, vl // bn),
-        grid=(t // bm, vl // bn),
-        in_specs=[pl.BlockSpec((bm, d), lambda i, v: (i, 0)), pl.BlockSpec((d, bn), lambda i, v: (0, v))],
-        out_specs=[pl.BlockSpec((bm, bn), lambda i, v: (i, v)), stat, stat],
-        out_shape=[jax.ShapeDtypeStruct((t, vl), F32), stat_shape, stat_shape],
-        scratch_shapes=[pltpu.VMEM((bm, 128), F32), pltpu.VMEM((bm, 128), F32)],
-        compiler_params=pltpu.CompilerParams(vmem_limit_bytes=VMEM_CAP),
+        functools.partial(gather_logits_kernel, nv),
+        grid=(4 * nv,),
+        in_specs=[hbm, pl.BlockSpec((d, bn), lambda i: (0, lax.rem(i, nv)))],
+        out_specs=[hbm, hbm, stat, stat],
+        out_shape=[jax.ShapeDtypeStruct((t, d), BF16), jax.ShapeDtypeStruct((t, vl), F32), stat_shape, stat_shape],
+        scratch_shapes=[
+            pltpu.VMEM((2, bm, d), BF16),
+            pltpu.VMEM((2, bm, bn), F32),
+            pltpu.VMEM((bm, 128), F32),
+            pltpu.VMEM((bm, 128), F32),
+            pltpu.SemaphoreType.DMA((12,)),
+            pltpu.SemaphoreType.DMA((12,)),
+            pltpu.SemaphoreType.DMA((2, 4)),
+            pltpu.SemaphoreType.DMA,
+            pltpu.SemaphoreType.DMA((2, 4)),
+        ],
+        compiler_params=pltpu.CompilerParams(
+            vmem_limit_bytes=VMEM_CAP, collective_id=2, has_side_effects=True
+        ),
         cost_estimate=pl.CostEstimate(flops=2 * t * d * vl, bytes_accessed=4 * t * vl, transcendentals=0),
-        name="logits_fwd",
-    )(h, w)
+        name="gather_logits",
+    )(h_own, w)
 
 
 def exchange_kernel(n, post, n_out, x_ref, *rest):
@@ -150,7 +312,7 @@
     misc_ref[8:16, :] = jnp.full((8, 128), jnp.sum(mask * (top + jnp.log(tot))), F32)
 
 
-def grad_h_kernel(nk, nn, z_ref, m_ref, a_ref, lab_ref, inv_ref, w_ref, *rest):
+def grad_h_kernel(nk, me_ref, z_ref, m_ref, a_ref, lab_ref, inv_ref, w_ref, *rest):
     dh_ref, dz_ref, t_ref, dz_s = rest[-4:]
     i = pl.program_id(0)
     groups, _, rows, bk = z_ref.shape
@@ -164,17 +326,18 @@
         hit_sum = jnp.zeros((STRIP, 128), F32)
         lanes = [(lane + (i * bk + 128 * j)).astype(F32) for j in range(bk // 128)]
         for grp in range(groups):
+            slot = lax.bitwise_xor(me_ref[0], grp)
             for r in range(0, rows, STRIP):
                 part = slice(r, r + STRIP)
                 m, a, lab = m_ref[grp, 0, part], a_ref[grp, 0, part], lab_ref[grp, 0, part]
                 for j in range(bk // 128):
                     cols = slice(128 * j, 128 * (j + 1))
-                    z = z_ref[grp, 0, part, cols]
+                    z = z_ref[slot, 0, part, cols]
                     hit = lab == lanes[j]
                     hit_sum = hit_sum + jnp.where(hit, z, 0.0)
                     dz = (jnp.exp(z - m) * a - jnp.where(hit, inv, 0.0)).astype(BF16)
                     dz_s[i, grp * rows + r : grp * rows + r + STRIP, cols] = dz
-                    dz_ref[grp, 0, part, cols] = dz
+                    dz_ref[slot, 0, part, cols] = dz
         for r in range(0, STRIP, 8):
             t_ref[...] += hit_sum[r : r + 8]
 
@@ -203,7 +366,7 @@
         product()
 
 
-def grad_h_chunk(z4, m4, a4, lab4, inv, w, dz4, c):
+def grad_h_chunk(me, z4, m4, a4, lab4, inv, w, dz4, c):
     groups, _, rows, vl = z4.shape
     d = w.shape[0]
     bn, bk = 1024, 1280
@@ -212,15 +375,15 @@
     tile = pl.BlockSpec((groups, 1, rows, bk), lambda i: (0, c, 0, jnp.minimum(i, nk - 1)))
     col = pl.BlockSpec((groups, 1, rows, 128), lambda i: (0, c, 0, 0))
     small = pl.BlockSpec((8, 128), lambda i: (0, 0))
-    in_specs = [tile, col, col, col, small, pl.BlockSpec((bn, bk), lambda i: (jnp.maximum(i - 1, 0) // nk, lax.rem(jnp.maximum(i - 1, 0), nk)))]
-    args = [z4, m4, a4, lab4, inv, w]
+    in_specs = [pl.BlockSpec(memory_space=pltpu.SMEM), tile, col, col, col, small, pl.BlockSpec((bn, bk), lambda i: (jnp.maximum(i - 1, 0) // nk, lax.rem(jnp.maximum(i - 1, 0), nk)))]
+    args = [me, z4, m4, a4, lab4, inv, w]
     aliases = {}
     if dz4 is not None:
         in_specs.append(pl.BlockSpec(memory_space=pl.ANY))
         aliases = {len(args): 1}
         args.append(dz4)
     return pl.pallas_call(
-        functools.partial(grad_h_kernel, nk, nn),
+        functools.partial(grad_h_kernel, nk),
         grid=(nk * nn + 1,),
         in_specs=in_specs,
         out_specs=[pl.BlockSpec((t, bn), lambda i: (0, jnp.maximum(i - 1, 0) // nk)), tile, small],
@@ -316,8 +479,17 @@
         x = hidden.reshape(rows, d)
         g = norm_gain.reshape(1, d)
         h_own = norm_fwd(x, g, norm_bias.reshape(1, d))
-        h = lax.all_gather(h_own, "vp", axis=0, tiled=True)
-        z, m_loc, s_loc_sum = logits_fwd(h, w)
+        h, z, m_slot, s_slot = gather_logits(h_own, w, n)
+        me = lax.axis_index("vp")
+        me_arr = me.reshape(1)
+
+        def by_device(v):
+            v = v.reshape(2, 2, 2, t // 128 // n, 128)
+            for axis, bit in ((0, 4), (1, 2), (2, 1)):
+                v = jnp.where((me & bit) != 0, jnp.flip(v, axis), v)
+            return v.reshape(t // 128, 128)
+
+        m_loc, s_loc_sum = by_device(m_slot), by_device(s_slot)
 
         lab_own = jnp.where(loss_mask > 0.0, labels, -1).astype(F32).reshape(nc, 128)
         stat_rows = t // 128
@@ -331,7 +503,7 @@
             0,
             "stats_exchange",
         )
-        col_start = (lax.axis_index("vp") * vl).astype(F32)
+        col_start = (me * vl).astype(F32)
 
         def wide(v):
             return jnp.broadcast_to(v[:, :, None], (stat_rows, 128, 128)).reshape(n, nc, 128, 128)
@@ -341,7 +513,7 @@
         inv = misc[:8]
         dz4, dhs, hits = None, [], []
         for c in range(nc):
-            dh_c, dz4, hit = grad_h_chunk(z4, m4, a4, lab4, inv, w, dz4, c)
+            dh_c, dz4, hit = grad_h_chunk(me_arr, z4, m4, a4, lab4, inv, w, dz4, c)
             hits.append(hit)
             dhs.append(lax.psum_scatter(dh_c, "vp", scatter_dimension=0, tiled=True))
         grad_w = grad_w_call(h, dz4.reshape(t, vl))

time: 1020 us -> 898 us (0.88)
  waiting for transfers between devices: 157 us -> 0.61 us
  Pallas kernels: 817 us -> 853 us
    all_gather x1 -> x0, waiting for transfers between devices: 156 us -> none  [per_device(): h = lax.all_gather(h_own, 'vp', axis=0, tiled=True)]
    pallas_call x5, Pallas kernels: 545 us -> 580 us  [the longest x4 312 us: grad_h_chunk(): pl.pallas_call(functools.partial(grad_h_kernel, nk), grid=(nk * nn + 1,),...]
  transfers between devices with their start and end apart: 5 -> 4, of which waited for: 1 -> 0; matrix products, arithmetic and copies ran while one was open for 0% -> 0% of each run, Pallas kernels for 46% -> 53%
where the time goes in v2:
time: 898 us; the launch traced here: 889 us
  Pallas kernels  853 us (95%)
  between operations  17.1 us (2%)
  local copies, waits for them, and re-layouts  13.1 us (1%)
    pallas_call x4, Pallas kernels, grad_h_chunk(): pl.pallas_call(functools.partial(grad_h_kernel, nk), grid=(nk * nn + 1,),...  312 us
    pallas_call x1, Pallas kernels, gather_logits(): pl.pallas_call(functools.partial(gather_logits_kernel, nv), grid=(4 * nv,...  267 us
    pallas_call x1, Pallas kernels, grad_w_call(): pl.pallas_call(grad_w_kernel, grid=(vl // bn, d // bm), in_specs=[pl.Bloc...  233 us
  transfers between devices with their start and end apart: 4, of which 0 were waited for; matrix products, arithmetic and copies ran while one was open for 0% of the time, Pallas kernels for 53%

profile of v2, /device:TPU:0, one launch (start us, length us, event | category | flops | bytes accessed | tf_op | source)
XLA Modules:
  0.0 888.9 jit_solution(11257901314028800930)
XLA Ops:
  7.2 0.0 reduce-scatter.5.cloned.1.call-start
  7.2 0.7 select_convert_fusion
  8.0 0.7 reshape.82
  8.6 7.0 norm_fwd.1.own_ref
  15.6 0.0 copy-start.1
  15.6 267.5 %gather_logits.1 = (bf16[4096,4096]{1,0:T(8,128)(2,1)}, f32[4096,6400]{1,0:T(8,128)}, f32[32,128]{1,0:T(8,128)}, f32[32,128]{1,0:T(8,128)}) custom-call(bf16[512,4096]{1,0:T(8,128)(2,1)} %norm_fwd.1.own_ref, bf16[4096,6400]{1,0:T(8,128)(2,1)} %w_ref.9), custom_call_target="tpu_custom_call" | custom-call | flops 214748364800 | bytes 104857600 | tf_op jit(solution)/shard_map/gather_logits/pallas_call | solution.py:230
  283.1 0.8 reverse_select_fusion.2
  284.0 0.1 pad.5.clone
  284.1 0.0 copy-done.1
  284.1 0.7 maximum_maximum_fusion.x_ref
  284.8 8.9 %stats_exchange.1 = (f32[32,128]{1,0:T(8,128)}, f32[32,128]{1,0:T(8,128)}, f32[32,128]{1,0:T(8,128)}, f32[16,128]{1,0:T(8,128)}) custom-call(f32[72,128]{1,0:T(8,128)} %maximum_maximum_fusion.x_ref), custom_call_target="tpu_custom_call" | custom-call | tf_op jit(solution)/shard_map/stats_exchange/pallas_call | solution.py:282
  293.7 1.3 slice.21.inv_ref
  295.0 0.7 broadcast_subtract_fusion
  295.7 1.9 broadcast_in_dim.38.lab_ref
  297.7 2.6 broadcast_in_dim.36.a_ref
  300.3 2.6 broadcast_in_dim.34.m_ref
  302.9 77.9 %grad_h.4 = (f32[1024,4096]{1,0:T(8,128)}, bf16[8,4,128,6400]{3,2,1,0:T(8,128)(2,1)}, f32[8,128]{1,0:T(8,128)}) custom-call(s32[1]{0:T(128)} %bitcast.7.me_ref, f32[8,4,128,6400]{3,2,1,0:T(8,128)} %bitcast.8.z_ref, f32[8,4,128,128]{3,2,1,0:T(8,128)} %broadcast_in_dim.34.m_ref, f32[8,4,128,128]{3,2,1,0:T(8,128)} %broadcast_in_dim.36.a_ref, ...), custom_call_target="tpu_custom_call" | custom-call | flops 53687091200 | bytes 26214400 | tf_op jit(solution)/shard_map/grad_h/pallas_call | solution.py:385
  380.8 0.0 reduce-scatter.5.cloned.1.call-update
  380.9 0.0 reduce-scatter.7.cloned.1.call-start
  380.9 78.0 %grad_h.5 = (f32[1024,4096]{1,0:T(8,128)}, bf16[8,4,128,6400]{3,2,1,0:T(8,128)(2,1)}, f32[8,128]{1,0:T(8,128)}) custom-call(s32[1]{0:T(128)} %bitcast.7.me_ref, f32[8,4,128,6400]{3,2,1,0:T(8,128)} %bitcast.8.z_ref, f32[8,4,128,128]{3,2,1,0:T(8,128)} %broadcast_in_dim.34.m_ref, ...), custom_call_target="tpu_custom_call", output_to_operand_aliasing={{1}: (7, {})} | custom-call | flops 53687091200 | bytes 26214400 | tf_op jit(solution)/shard_map/grad_h/pallas_call | solution.py:385
  458.9 0.0 reduce-scatter.7.cloned.1.call-update
  459.0 0.0 reduce-scatter.11.cloned.1.call-start
  459.0 78.1 %grad_h.6 = (f32[1024,4096]{1,0:T(8,128)}, bf16[8,4,128,6400]{3,2,1,0:T(8,128)(2,1)}, f32[8,128]{1,0:T(8,128)}) custom-call(s32[1]{0:T(128)} %bitcast.7.me_ref, f32[8,4,128,6400]{3,2,1,0:T(8,128)} %bitcast.8.z_ref, f32[8,4,128,128]{3,2,1,0:T(8,128)} %broadcast_in_dim.34.m_ref, ...), custom_call_target="tpu_custom_call", output_to_operand_aliasing={{1}: (7, {})} | custom-call | flops 53687091200 | bytes 26214400 | tf_op jit(solution)/shard_map/grad_h/pallas_call | solution.py:385
  537.1 78.4 %grad_h.7 = (f32[1024,4096]{1,0:T(8,128)}, bf16[8,4,128,6400]{3,2,1,0:T(8,128)(2,1)}, f32[8,128]{1,0:T(8,128)}) custom-call(s32[1]{0:T(128)} %bitcast.7.me_ref, f32[8,4,128,6400]{3,2,1,0:T(8,128)} %bitcast.8.z_ref, f32[8,4,128,128]{3,2,1,0:T(8,128)} %broadcast_in_dim.34.m_ref, ...), custom_call_target="tpu_custom_call", output_to_operand_aliasing={{1}: (7, {})} | custom-call | flops 53687091200 | bytes 26214400 | tf_op jit(solution)/shard_map/grad_h/pallas_call | solution.py:385
  615.5 0.0 copy-start.2
  615.5 0.0 copy-start.3
  615.5 0.0 copy-start.4
  615.6 0.0 copy-start.5
  615.6 0.0 reduce-scatter.11.cloned.1.call-update
  615.6 0.0 reduce-scatter.9.cloned.1.call-start
  615.6 0.5 reduce-scatter.9.cloned.1.call-update
  616.2 1.2 fusion
  617.4 0.0 copy-done.2
  617.4 0.0 copy-done.3
  617.4 0.0 copy-done.4
  617.4 0.0 copy-done.5
  617.4 0.6 add_add_fusion
  618.0 0.0 copy-start
  618.0 233.1 %grad_w.1 = f32[4096,6400]{1,0:T(8,128)} custom-call(bf16[4096,4096]{1,0:T(8,128)(2,1)} %get-tuple-element.50.h_ref, bf16[4096,6400]{1,0:T(8,128)(2,1)} %bitcast.21), custom_call_target="tpu_custom_call" | custom-call | flops 214748364800 | bytes 104857600 | tf_op jit(solution)/shard_map/grad_w/pallas_call | solution.py:411
  851.1 0.0 reduce-scatter.5.cloned.1.call-done.rest_0_
  851.1 0.0 reduce-scatter.7.cloned.1.call-done.rest_1_
  851.1 0.0 reduce-scatter.11.cloned.1.call-done.rest_3_
  851.1 0.0 reduce-scatter.9.cloned.1.call-done.rest_2_
  851.2 15.6 %norm_bwd.1 = (bf16[512,4096]{1,0:T(8,128)(2,1)}, f32[16,4096]{1,0:T(8,128)}) custom-call(bf16[512,4096]{1,0:T(8,128)(2,1)} %bitcast.23, f32[1,4096]{1,0:T(1,128)} %bitcast.25, f32[128,4096]{1,0:T(8,128)} %reduce-scatter.5.cloned.1.call-done.rest_0_, f32[128,4096]{1,0:T(8,128)} %reduce-scatter.7.cloned.1.call-done.rest_1_, ...), custom_call_target="tpu_custom_call" | custom-call | tf_op jit(solution)/shard_map/norm_bwd/pallas_call | solution.py:452
  866.7 1.0 bitcast_reduce_fusion
  867.8 0.0 copy-done
  867.8 0.6 pad_maximum_fusion.x_ref
  868.5 8.1 final_exchange.1
  876.6 1.2 slice.22
  877.8 1.3 slice_bitcast_fusion
  (6 shorter events, 0.1 us)
Async XLA Ops:
  7.2 843.9 %reduce-scatter.5.cloned.1.call-start = ((), (), s32[]{:S(2)}) async-start(), calls=%async_computation.4 | async-start | bytes 18874368 | tf_op jit(solution)/shard_map/reduce_scatter | solution.py:518
  15.6 268.5 %copy-start.1 = (f32[4,128]{1,0:T(4,128)S(1)}, f32[4,128]{1,0:T(4,128)}, u32[]{:S(2)}) copy-start(f32[4,128]{1,0:T(4,128)} %reshape.82) | copy-start | bytes 6148
  380.9 470.2 %reduce-scatter.7.cloned.1.call-start = ((), (), s32[]{:S(2)}) async-start(), calls=%async_computation.5 | async-start | bytes 18874368 | tf_op jit(solution)/shard_map/reduce_scatter | solution.py:518
  459.0 392.2 %reduce-scatter.11.cloned.1.call-start = ((), (), s32[]{:S(2)}) async-start(), calls=%async_computation.7 | async-start | bytes 18874368 | tf_op jit(solution)/shard_map/reduce_scatter | solution.py:518
  615.5 1.9 copy-start.2
  615.5 1.9 copy-start.3
  615.5 1.8 copy-start.4
  615.6 1.8 copy-start.5
  615.6 235.6 %reduce-scatter.9.cloned.1.call-start = ((), (), s32[]{:S(2)}) async-start(), calls=%async_computation.6 | async-start | bytes 18874368 | tf_op jit(solution)/shard_map/reduce_scatter | solution.py:518
  618.0 249.8 %copy-start = (f32[8,128]{1,0:T(8,128)S(1)}, f32[8,128]{1,0:T(8,128)}, u32[]{:S(2)}) copy-start(f32[8,128]{1,0:T(8,128)} %add_add_fusion) | copy-start | bytes 12292
Sparse Core Ops, SparseCore 0:
  381.0 107.1 reduce-scatter.4
  491.6 106.9 reduce-scatter.6
  615.7 107.1 reduce-scatter.10
  726.2 106.9 reduce-scatter.8
